TPU v7x, 128 devices: a whole 4x4x4 slice. The times are simulated.
128 devices in a mesh: data: 1, seq: 128 (over z, y, x, core).
Axes of the slice: x: 4, y: 4, z: 4, core: 2. Of those that a mesh axis runs over, the one named last changes fastest.
Arguments:
- tokens: bfloat16 [32, 16384, 384], P('data', 'seq')
- lengths: int32 [32], P('data')
- slot_params: bfloat16 [384, 128], replicated
- logit_scale: float32 [1], replicated
- w_in: bfloat16 [128, 384, 1536], P('seq')
- w_out: bfloat16 [128, 1536, 384], P('seq')
Outputs:
- output: bfloat16 [32, 16384, 384], P('data', 'seq')
All inputs are finite; a program needn't handle non-finite values.
Results may differ from a plain program's by a relative error of at most 0.0157012.
Values are sent between devices in bfloat16 or wider.
A program may use at most 1 GiB of HBM per device.

v0:
```python
import jax
import jax.numpy as jnp
from jax import lax
from jax.sharding import PartitionSpec as P


def solution(mesh):
    seq_size = mesh.shape["seq"]

    def shard_body(tok_blk, len_blk, slot_params, logit_scale, w_in_blk, w_out_blk):
        num_rows, tok_count, model_width = tok_blk.shape
        num_slots = slot_params.shape[1]
        own_slots = num_slots // seq_size
        local_experts = w_in_blk.shape[0]
        slots_per = own_slots // local_experts
        shard_idx = lax.axis_index("seq")
        params_f32 = slot_params.astype(jnp.float32)
        col_inv = lax.rsqrt(jnp.sum(params_f32 * params_f32, axis=0, keepdims=True) + 1e-6)
        phi_norm = (params_f32 * (logit_scale[0] * col_inv)).astype(jnp.bfloat16)
        tok_f32 = tok_blk.astype(jnp.float32)
        tok_norm = (tok_f32 * lax.rsqrt(jnp.sum(tok_f32 * tok_f32, axis=-1, keepdims=True) + 1e-6)).astype(jnp.bfloat16)
        logits = jnp.einsum("btd,dn->btn", tok_norm, phi_norm, preferred_element_type=jnp.float32)
        positions = shard_idx * tok_count + jnp.arange(tok_count)
        is_valid = (positions[None, :] < len_blk[:, None])[:, :, None]
        local_max = jnp.max(jnp.where(is_valid, logits, -jnp.inf), axis=1)
        col_max = lax.pmax(local_max, "seq")
        disp_w = jnp.where(is_valid, jnp.exp(logits - col_max[:, None, :]), 0.0)
        col_sum = lax.psum(jnp.sum(disp_w, axis=1), "seq")
        part_sum = jnp.einsum("btn,btd->bnd", disp_w.astype(jnp.bfloat16), tok_blk, preferred_element_type=jnp.float32).astype(jnp.bfloat16)
        slot_sum = lax.psum_scatter(part_sum, "seq", scatter_dimension=1, tiled=True)
        own_sum = lax.dynamic_slice_in_dim(col_sum, shard_idx * own_slots, own_slots, axis=1)
        slot_in = (slot_sum.astype(jnp.float32) / own_sum[:, :, None]).astype(jnp.bfloat16)
        slot_in = slot_in.reshape(num_rows, local_experts, slots_per, model_width)
        hidden = jax.nn.gelu(jnp.einsum("besd,edf->besf", slot_in, w_in_blk, preferred_element_type=jnp.float32)).astype(jnp.bfloat16)
        slot_out = jnp.einsum("besf,efd->besd", hidden, w_out_blk, preferred_element_type=jnp.float32).astype(jnp.bfloat16)
        slot_out = slot_out.reshape(num_rows, own_slots, model_width)
        all_out = lax.all_gather(slot_out, "seq", axis=1, tiled=True)
        combine_w = jax.nn.softmax(logits, axis=-1).astype(jnp.bfloat16)
        mixed = jnp.einsum("btn,bnd->btd", combine_w, all_out, preferred_element_type=jnp.float32).astype(jnp.bfloat16)
        return jnp.where(is_valid, mixed, jnp.zeros_like(mixed))

    return jax.shard_map(
        shard_body,
        mesh=mesh,
        in_specs=(P("data", "seq", None), P("data"), P(None, None), P(None), P("seq", None, None), P("seq", None, None)),
        out_specs=P("data", "seq", None),
        check_vma=False,
    )
```

profile of v0, /device:TPU:1, one launch (start us, length us, event | category | flops | bytes accessed | tf_op | source)
XLA Modules:
  0.0 378.2 jit_solution(15802669667741765477)
XLA Ops:
  6.5 0.0 copy-start
  6.5 0.0 copy-start.2
  6.5 0.0 copy-start.3
  6.5 0.0 reduce-scatter.2.cloned.1.call-start
  6.6 0.0 copy-start.1
  6.6 2.7 fusion.1
  10.0 0.0 copy-done.2
  10.0 0.1 fusion.27
  10.1 0.0 copy-done.3
  10.1 0.1 broadcast_compare_fusion
  10.1 0.0 copy-done.1
  10.1 1.3 select_reduce_fusion
  11.4 68.8 %pmax.7 = f32[32,128]{1,0:T(8,128)S(1)} all-reduce(f32[32,128]{1,0:T(8,128)S(1)} %get-tuple-element.5), channel_id=1, replica_groups=mesh['data'=1,'seq'=128] {'seq'}, use_global_device_ids=true, to_apply=%region_5.6 | all-reduce | flops 4096 | bytes 32768 | tf_op jit(solution)/shard_map/pmax | solution.py:26
  80.2 3.3 convolution_convert_fusion
  83.6 3.5 copy.15
  87.1 0.0 reduce-scatter.2.cloned.1.call-update
  87.1 0.0 all-gather.3.cloned.1.call-start
  87.1 0.7 fusion.11
  87.9 62.8 %psum.7 = f32[32,128]{1,0:T(8,128)S(1)} all-reduce(f32[32,128]{1,0:T(8,128)S(1)} %fusion.11), channel_id=1, replica_groups=mesh['data'=1,'seq'=128] {'seq'}, use_global_device_ids=true, to_apply=%region_8.9 | all-reduce | flops 4096 | bytes 32768 | tf_op jit(solution)/shard_map/psum | solution.py:28
  150.7 0.2 dynamic-slice_reduce_fusion
  150.9 141.1 %reduce-scatter.2.cloned.1.call-done = bf16[32,1,384]{2,0,1:T(8,128)(2,1)} async-done(((bf16[32,128,384]{2,0,1:T(8,128)(2,1)}), bf16[32,1,384]{2,0,1:T(8,128)(2,1)}) %reduce-scatter.2.cloned.1.call-update) | async-done | bytes 24592 | tf_op jit(solution)/shard_map/reduce_scatter | solution.py:30
  292.0 0.0 copy-done
  292.0 2.5 fusion.19
  294.5 0.0 all-gather.3.cloned.1.call-update
  294.5 1.2 fusion.64
  295.7 65.2 %all-gather.3.cloned.1.call-done = bf16[32,128,1,384]{3,0,2,1:T(8,128)(2,1)} async-done(((bf16[32,1,1,384]{3,0,2,1:T(8,128)(2,1)}), bf16[32,128,1,384]{3,0,2,1:T(8,128)(2,1)}) %all-gather.3.cloned.1.call-update) | async-done | bytes 3145744 | tf_op jit(solution)/shard_map/all_gather | solution.py:37
  360.9 10.4 %convert_select_fusion = bf16[32,128,384]{2,1,0:T(8,128)(2,1)} fusion(pred[32,128]{1,0:T(8,128)(4,1)S(1)} %broadcast_compare_fusion, bf16[32,128,1,384]{3,0,2,1:T(8,128)(2,1)} %all-gather.3.cloned.1.call-done, f32[32,128]{1,0:T(8,128)S(1)} %fusion.64, f32[32,128,128]{2,1,0:T(8,128)S(1)} %get-tuple-element.6), kind=kOutput, calls=%fused_computation.9 | convolution fusion | flops 407376000 | bytes 8409088 | tf_op jit(solution)/shard_map/btn,bnd->btd/dot_general | solution.py:39
  (3 shorter events, 0.0 us)
Async XLA Ops:
  6.5 285.5 %copy-start = (bf16[1,1536,384]{2,1,0:T(8,128)(2,1)S(1)}, bf16[1,1536,384]{2,1,0:T(8,128)(2,1)}, u32[]{:S(2)}) copy-start(bf16[1,1536,384]{2,1,0:T(8,128)(2,1)} %param.11) | copy-start | bytes 3538948
  6.5 3.4 copy-start.2
  6.5 3.5 copy-start.3
  6.5 285.4 %reduce-scatter.2.cloned.1.call-start = ((), (), s32[]{:S(2)}) async-start(), calls=%async_computation.1 | async-start | bytes 3170304 | tf_op jit(solution)/shard_map/reduce_scatter | solution.py:30
  6.6 3.6 copy-start.1
  87.1 273.8 %all-gather.3.cloned.1.call-start = ((), (), s32[]{:S(2)}) async-start(), calls=%async_computation.2 | async-start | bytes 3170304 | tf_op jit(solution)/shard_map/all_gather | solution.py:37
Sparse Core Ops, SparseCore 0:
  87.2 204.7 reduce-scatter.1
  295.1 65.7 all-gather.2
where the time goes:
time: 379 us; the launch traced here: 378 us
  waiting for transfers between devices  206 us (54%)
  blocking collectives  132 us (35%)
  matrix products  17.5 us (5%)
  between operations  14.1 us (4%)
  other arithmetic  4.8 us (1%)
    reduce_scatter x1, waiting for transfers between devices, shard_body(): lax.psum_scatter(part_sum, 'seq', scatter_dimension=1, tiled=True)  141 us
    pmax x1, blocking collectives, shard_body(): col_max = lax.pmax(local_max, 'seq')  68.8 us
    all_gather x1, waiting for transfers between devices, shard_body(): all_out = lax.all_gather(slot_out, 'seq', axis=1, tiled=True)  65.2 us
    psum x1, blocking collectives, shard_body(): col_sum = lax.psum(jnp.sum(disp_w, axis=1), 'seq')  62.8 us
    dot_general x1, matrix products, shard_body(): jnp.einsum('btn,bnd->btd', combine_w, all_out, preferred_element_type=jnp...  10.4 us
  transfers between devices with their start and end apart: 2, of which 2 were waited for; matrix products, arithmetic and copies ran while one was open for 1% of the time, Pallas kernels for 0%

commit v1 on v0

v1 whole, which is shorter than its diff:
```python
import functools

import jax
import jax.numpy as jnp
from jax import lax
from jax.experimental import pallas as pl
from jax.experimental.pallas import tpu as pltpu
from jax.sharding import PartitionSpec as P

F32, BF16 = jnp.float32, jnp.bfloat16
COLOR_ROWS = (11, 11, 10)
COLOR_START = (0, 11, 22)
COLOR_HALF = (6, 6, 5)
STRIDE = {"z": 32, "y": 8, "x": 2}
COLOR_AXES = (("z", "y", "x"), ("y", "x", "z"), ("x", "z", "y"))
COPIES = 160


def slots_kernel(
    len_ref, scale_ref, tok_hbm, phi_ref, win_hbm, wout_hbm,
    comb_hbm, gat_hbm,
    tok, win, wout, comb, part, swap, chip, relay, line,
    two_out, two_in, three_out, three_in, z_own, z_out, z_swap, z_in, lanes, gat,
    send_sem, recv_sem, local_sem,
):
    num_rows, tok_count, width = tok.shape
    me = lax.axis_index("seq")
    core = lax.rem(me, 2)
    at = {axis: lax.rem(lax.div(me, stride), 4) for axis, stride in STRIDE.items()}
    partner = me + 1 - 2 * core

    def peer(axis, step):
        return me + (lax.rem(at[axis] + step, 4) - at[axis]) * STRIDE[axis]

    copies = []

    def push(src, dst, device):
        index = len(copies)
        copy = pltpu.make_async_remote_copy(
            src_ref=src, dst_ref=dst, send_sem=send_sem.at[index], recv_sem=recv_sem.at[index],
            device_id={"seq": device}, device_id_type=pl.DeviceIdType.MESH,
        )
        copy.start()
        copies.append(copy)
        return copy

    chunks = []
    for half in range(2):
        for color in range(3):
            start, rows, cut = COLOR_START[color], COLOR_ROWS[color], COLOR_HALF[color]
            chunks.append((color, half, start + half * cut, cut if half == 0 else rows - cut))

    barrier = pltpu.get_barrier_semaphore()
    neighbours = [partner] + [peer(axis, step) for axis in STRIDE for step in (1, 2, 3)]
    for other in neighbours:
        pl.semaphore_signal(barrier, inc=1, device_id={"seq": other}, device_id_type=pl.DeviceIdType.MESH)

    loads = []
    for index, (_, _, lo, count) in enumerate(chunks):
        load = pltpu.make_async_copy(tok_hbm.at[pl.ds(lo, count)], tok.at[pl.ds(lo, count)], local_sem.at[index])
        load.start()
        loads.append(load)
    load_in = pltpu.make_async_copy(win_hbm.at[0], win, local_sem.at[6])
    load_out = pltpu.make_async_copy(wout_hbm.at[0], wout, local_sem.at[7])
    load_in.start()
    load_out.start()

    params = phi_ref[...].astype(F32)
    col_inv = lax.rsqrt(jnp.sum(params * params, axis=0, keepdims=True) + 1e-6)
    phi = (params * (scale_ref[0] * col_inv)).astype(BF16)
    slot = lax.broadcasted_iota(jnp.int32, (128, 128), 0)
    place = lax.broadcasted_iota(jnp.int32, (128, 128), 1)
    phis = []
    for color in range(3):
        owner = (core + (place >> 6)) & 1
        for depth, axis in enumerate(COLOR_AXES[color]):
            owner = owner + STRIDE[axis] * ((at[axis] + (place >> (4 - 2 * depth))) & 3)
        pick = jnp.where(slot == owner, 1.0, 0.0).astype(BF16)
        phis.append(jnp.dot(phi, pick, preferred_element_type=F32).astype(BF16))
    z_own[...] = jnp.ones_like(z_own)
    position = me * tok_count + lax.broadcasted_iota(jnp.int32, (tok_count, 128), 0)

    def dispatch(chunk):
        color, _, lo, count = chunk

        def body(step, carry):
            row = lo + step
            x = tok[row]
            xf = x.astype(F32)
            inv = lax.rsqrt(jnp.sum(xf * xf, axis=-1, keepdims=True) + 1e-6)
            logits = jnp.dot((xf * inv).astype(BF16), phis[color], preferred_element_type=F32)
            weight = jnp.exp(logits)
            comb[row] = (weight / jnp.sum(weight, axis=-1, keepdims=True)).astype(BF16)
            weight = jnp.where(position < len_ref[row], weight, 0.0)
            z_own[color, pl.ds(row - COLOR_START[color], 1), :] = jnp.sum(weight, axis=0, keepdims=True)
            total = lax.dot_general(
                weight.astype(BF16), x, (((0,), (0,)), ((), ())), preferred_element_type=F32
            ).astype(BF16)
            part[row, 0] = total[:64]
            part[row, 1] = total[64:]
            return carry

        lax.fori_loop(0, count, body, 0)

    def start_swap(chunk):
        color, half, lo, count = chunk
        rows = pl.ds(lo, count)
        out = [push(part.at[rows, 1], swap.at[rows], partner)]
        if half == 1:
            z_out[0, color] = pltpu.roll(z_own[color], 64, 1)
            out.append(push(z_out.at[0, color], z_swap.at[color], partner))
        return out

    def line_z(color, phase, total):
        z_out[phase, color] = total
        axis = COLOR_AXES[color][phase - 1]
        return [push(z_out.at[phase, color], z_in.at[phase - 1, color, step - 1], peer(axis, step)) for step in (1, 2, 3)]

    def sum_z(color, phase, arrivals):
        total = z_out[phase, color]
        for step in (1, 2, 3):
            arrivals[step - 1].wait_recv()
            shift = 128 - step * (64 >> (2 * phase))
            total = total + pltpu.roll(z_in[phase - 1, color, step - 1], shift, 1)
        return total

    relays, cleans, z_one = {}, {}, {}

    def start_line(chunk, arrivals):
        color, half, lo, count = chunk
        for copy in arrivals:
            copy.wait_recv()

        def body(step, carry):
            row = lo + step
            both = part[row, 0].astype(F32) + swap[row].astype(F32)
            chip[row] = both.astype(BF16).reshape(4, 16, width)
            return carry

        lax.fori_loop(0, count, body, 0)
        rows = pl.ds(lo, count)
        axis = COLOR_AXES[color][0]
        away, back = (1, 3) if half == 0 else (3, 1)
        relays[color, half] = push(chip.at[rows, 2], relay.at[rows], peer(axis, away))
        cleans[color, half] = push(chip.at[rows, back], line.at[half, rows], peer(axis, back))
        if half == 1:
            z_one[color] = line_z(color, 1, z_own[color] + z_swap[color])

    for chunk, load in zip(chunks[:1], loads[:1]):
        load.wait()
        dispatch(chunk)
    pl.semaphore_wait(barrier, len(neighbours))
    pending = start_swap(chunks[0])
    for index in range(len(chunks)):
        following = None
        if index + 1 < len(chunks):
            loads[index + 1].wait()
            dispatch(chunks[index + 1])
            following = start_swap(chunks[index + 1])
        start_line(chunks[index], pending)
        pending = following
    store_comb = pltpu.make_async_copy(comb, comb_hbm, local_sem.at[8])
    store_comb.start()

    seconds = {}
    for chunk in chunks:
        color, half, lo, count = chunk
        axis = COLOR_AXES[color][0]
        relays[color, half].wait_recv()
        away = 1 if half == 0 else 3

        def body(step, carry):
            row = lo + step
            chip[row, away] = (chip[row, away].astype(F32) + relay[row].astype(F32)).astype(BF16)
            return carry

        lax.fori_loop(0, count, body, 0)
        rows = pl.ds(lo, count)
        seconds[color, half] = push(chip.at[rows, away], line.at[1 - half, rows], peer(axis, away))

    left = lax.broadcasted_iota(jnp.int32, (256, 256), 0)
    right = lax.broadcasted_iota(jnp.int32, (256, 256), 1)
    turn = jnp.where(((left >> 4) == (right & 15)) & ((left & 15) == (right >> 4)), 1.0, 0.0).astype(BF16)

    twos, z_two = {}, {}
    for color in range(3):
        rows, start = COLOR_ROWS[color], COLOR_START[color]
        span = pl.ds(start, rows)
        for half in range(2):
            cleans[color, half].wait_recv()
            seconds[color, half].wait_recv()
        z_two[color] = line_z(color, 2, sum_z(color, 1, z_one[color]))
        total = chip[span, 0].astype(F32) + line[0, span].astype(F32) + line[1, span].astype(F32)
        total = total.astype(BF16).reshape(rows * 16, width)
        turned = jnp.dot(turn[:, : rows * 16], total, preferred_element_type=F32)
        two_out[color] = turned.astype(BF16).reshape(4, 4, 16, width)
        axis = COLOR_AXES[color][1]
        twos[color] = [push(two_out.at[color, step], two_in.at[color, step - 1], peer(axis, step)) for step in (1, 2, 3)]

    threes, z_three = {}, {}
    for color in range(3):
        z_three[color] = line_z(color, 3, sum_z(color, 2, z_two[color]))
        total = two_out[color, 0].astype(F32)
        for step in (1, 2, 3):
            twos[color][step - 1].wait_recv()
            total = total + two_in[color, step - 1].astype(F32)
        three_out[color] = total.astype(BF16)
        axis = COLOR_AXES[color][2]
        threes[color] = [push(three_out.at[color, step], three_in.at[color, step - 1], peer(axis, step)) for step in (1, 2, 3)]

    slot_in = []
    for color in range(3):
        z_sum = sum_z(color, 3, z_three[color])
        total = three_out[color, 0].astype(F32)
        for step in (1, 2, 3):
            threes[color][step - 1].wait_recv()
            total = total + three_in[color, step - 1].astype(F32)
        slot_in.append((total / z_sum[:, :1]).astype(BF16))
    slot_in = jnp.concatenate(slot_in, axis=0)

    load_in.wait()
    load_out.wait()
    slot_out = jnp.zeros((48, width), F32)
    for piece in range(3):
        cols = pl.ds(piece * 512, 512)
        hidden = jnp.dot(slot_in, win[:, cols], preferred_element_type=F32)
        hidden = jax.nn.gelu(hidden).astype(BF16)
        slot_out = slot_out + jnp.dot(hidden, wout[cols, :], preferred_element_type=F32)
    slot_out = slot_out.astype(BF16)

    firsts = {}
    for color in range(3):
        lanes[color, 0, 0] = slot_out[16 * color : 16 * color + 16]
        axis = COLOR_AXES[color][2]
        firsts[color] = [push(lanes.at[color, 0, 0], lanes.at[color, 0, 4 - step], peer(axis, step)) for step in (1, 2, 3)]
    nexts = {}
    for color in range(3):
        for copy in firsts[color]:
            copy.wait_recv()
        axis = COLOR_AXES[color][1]
        nexts[color] = [push(lanes.at[color, 0], lanes.at[color, 4 - step], peer(axis, step)) for step in (1, 2, 3)]

    outs, across = {}, {color: [] for color in range(3)}

    def halves(color):
        start, rows, cut = COLOR_START[color], COLOR_ROWS[color], COLOR_HALF[color]
        return pl.ds(start, cut), pl.ds(start + cut, rows - cut)

    for color in range(3):
        rows, start = COLOR_ROWS[color], COLOR_START[color]
        for copy in nexts[color]:
            copy.wait_recv()
        turned = jnp.dot(turn[: rows * 16], lanes[color].reshape(256, width), preferred_element_type=F32)
        gat[pl.ds(start, rows), 0, 0] = turned.astype(BF16).reshape(rows, 16, width)
        early, late = halves(color)
        axis = COLOR_AXES[color][0]
        up, down = peer(axis, 1), peer(axis, 3)
        outs[color] = [
            push(gat.at[early, 0, 0], gat.at[early, 0, 3], up),
            push(gat.at[late, 0, 0], gat.at[late, 0, 1], down),
            push(gat.at[late, 0, 0], gat.at[late, 0, 3], up),
            push(gat.at[early, 0, 0], gat.at[early, 0, 1], down),
        ]
        span = pl.ds(start, rows)
        across[color].append(push(gat.at[span, 0, 0], gat.at[span, 1, 0], partner))

    hops = {}
    for color in range(3):
        early, late = halves(color)
        axis = COLOR_AXES[color][0]
        up, down = peer(axis, 1), peer(axis, 3)
        outs[color][0].wait_recv()
        first = push(gat.at[early, 0, 3], gat.at[early, 0, 2], up)
        outs[color][1].wait_recv()
        second = push(gat.at[late, 0, 1], gat.at[late, 0, 2], down)
        hops[color] = [first, second]
        across[color].append(push(gat.at[early, 0, 3], gat.at[early, 1, 3], partner))
        across[color].append(push(gat.at[late, 0, 1], gat.at[late, 1, 1], partner))
    for color in range(3):
        early, late = halves(color)
        outs[color][2].wait_recv()
        across[color].append(push(gat.at[late, 0, 3], gat.at[late, 1, 3], partner))
        outs[color][3].wait_recv()
        across[color].append(push(gat.at[early, 0, 1], gat.at[early, 1, 1], partner))
    for color in range(3):
        early, late = halves(color)
        hops[color][0].wait_recv()
        across[color].append(push(gat.at[early, 0, 2], gat.at[early, 1, 2], partner))
        hops[color][1].wait_recv()
        across[color].append(push(gat.at[late, 0, 2], gat.at[late, 1, 2], partner))
    stores = [store_comb]
    for color in range(3):
        for copy in across[color]:
            copy.wait_recv()
        span = pl.ds(COLOR_START[color], COLOR_ROWS[color])
        store = pltpu.make_async_copy(gat.at[span], gat_hbm.at[span], local_sem.at[9 + color])
        store.start()
        stores.append(store)
    for copy in copies:
        copy.wait_send()
    for store in stores:
        store.wait()


def combine_kernel(len_ref, comb_ref, gat_ref, y_ref):
    count, tok_count, _ = comb_ref.shape
    base = pl.program_id(0) * count
    position = lax.axis_index("seq") * tok_count + lax.broadcasted_iota(jnp.int32, (tok_count, 1), 0)
    for step in range(count):
        mixed = jnp.dot(comb_ref[step], gat_ref[step], preferred_element_type=F32).astype(BF16)
        y_ref[step] = jnp.where(position < len_ref[base + step], mixed, jnp.zeros_like(mixed))


def solution(mesh):
    def shard_body(tok_blk, len_blk, slot_params, logit_scale, w_in_blk, w_out_blk):
        rows, toks, width = tok_blk.shape
        ff = w_in_blk.shape[2]
        slots = slot_params.shape[1]
        smem = pl.BlockSpec(memory_space=pltpu.SMEM)
        vmem = pl.BlockSpec(memory_space=pltpu.VMEM)
        hbm = pl.BlockSpec(memory_space=pl.ANY)
        comb, gat = pl.pallas_call(
            slots_kernel,
            name="slots",
            out_shape=(
                jax.ShapeDtypeStruct((rows, toks, slots), BF16),
                jax.ShapeDtypeStruct((rows, 2, 4, 16, width), BF16),
            ),
            in_specs=[smem, smem, hbm, vmem, hbm, hbm],
            out_specs=(hbm, hbm),
            scratch_shapes=[
                pltpu.VMEM((rows, toks, width), BF16),
                pltpu.VMEM((width, ff), BF16),
                pltpu.VMEM((ff, width), BF16),
                pltpu.VMEM((rows, toks, slots), BF16),
                pltpu.VMEM((rows, 2, 64, width), BF16),
                pltpu.VMEM((rows, 64, width), BF16),
                pltpu.VMEM((rows, 4, 16, width), BF16),
                pltpu.VMEM((rows, 16, width), BF16),
                pltpu.VMEM((2, rows, 16, width), BF16),
                pltpu.VMEM((3, 4, 4, 16, width), BF16),
                pltpu.VMEM((3, 3, 4, 16, width), BF16),
                pltpu.VMEM((3, 4, 16, width), BF16),
                pltpu.VMEM((3, 3, 16, width), BF16),
                pltpu.VMEM((3, 16, slots), F32),
                pltpu.VMEM((4, 3, 16, slots), F32),
                pltpu.VMEM((3, 16, slots), F32),
                pltpu.VMEM((3, 3, 3, 16, slots), F32),
                pltpu.VMEM((3, 4, 4, 16, width), BF16),
                pltpu.VMEM((rows, 2, 4, 16, width), BF16),
                pltpu.SemaphoreType.DMA((COPIES,)),
                pltpu.SemaphoreType.DMA((COPIES,)),
                pltpu.SemaphoreType.DMA((12,)),
            ],
            compiler_params=pltpu.CompilerParams(collective_id=0, has_side_effects=True, vmem_limit_bytes=60 * 1024 * 1024),
        )(len_blk, logit_scale, tok_blk, slot_params, w_in_blk, w_out_blk)
        gat = gat.reshape(rows, slots, width)
        block = 4
        return pl.pallas_call(
            combine_kernel,
            name="combine",
            out_shape=jax.ShapeDtypeStruct((rows, toks, width), BF16),
            grid=(rows // block,),
            in_specs=[
                smem,
                pl.BlockSpec((block, toks, slots), lambda i: (i, 0, 0)),
                pl.BlockSpec((block, slots, width), lambda i: (i, 0, 0)),
            ],
            out_specs=pl.BlockSpec((block, toks, width), lambda i: (i, 0, 0)),
        )(len_blk, comb, gat)

    return jax.shard_map(
        shard_body,
        mesh=mesh,
        in_specs=(P("data", "seq", None), P("data"), P(None, None), P(None), P("seq", None, None), P("seq", None, None)),
        out_specs=P("data", "seq", None),
        check_vma=False,
    )
```

time: 379 us -> 71.2 us (0.19)
  waiting for transfers between devices: 206 us -> 0 us
  blocking collectives: 132 us -> 0 us
  Pallas kernels: 0 us -> 70.2 us
  matrix products: 17.5 us -> 0 us
  between operations: 14.1 us -> 0.66 us
  other arithmetic: 4.8 us -> 0 us
    reduce_scatter x1 -> x0, waiting for transfers between devices: 141 us -> none  [shard_body(): lax.psum_scatter(part_sum, 'seq', scatter_dimension=1, tiled=True)]
    pallas_call x0 -> x2, Pallas kernels: none -> 70.2 us  [the longest x1 63 us: shard_body(): pl.pallas_call(slots_kernel, name='slots', out_shape=(jax.ShapeDtypeStruc...]
    pmax x1 -> x0, blocking collectives: 68.8 us -> none  [shard_body(): col_max = lax.pmax(local_max, 'seq')]
    all_gather x1 -> x0, waiting for transfers between devices: 65.2 us -> none  [shard_body(): all_out = lax.all_gather(slot_out, 'seq', axis=1, tiled=True)]
    psum x1 -> x0, blocking collectives: 62.8 us -> none  [shard_body(): col_sum = lax.psum(jnp.sum(disp_w, axis=1), 'seq')]
    dot_general x4 -> x0, matrix products: 17.5 us -> none  [the longest x1 10.4 us: shard_body(): jnp.einsum('btn,bnd->btd', combine_w, all_out, preferred_element_type=jnp...]
  transfers between devices with their start and end apart: 2 -> 0, of which waited for: 2 -> 0; matrix products, arithmetic and copies ran while one was open for 1% -> 0% of each run, Pallas kernels for 0% -> 0%
where the time goes in v1:
time: 71.2 us; the launch traced here: 70.9 us
  Pallas kernels  70.2 us (99%)
    pallas_call x1, Pallas kernels, shard_body(): pl.pallas_call(slots_kernel, name='slots', out_shape=(jax.ShapeDtypeStruc...  63 us
    pallas_call x1, Pallas kernels, shard_body(): pl.pallas_call(combine_kernel, name='combine', out_shape=jax.ShapeDtypeSt...  7.22 us

profile of v1, /device:TPU:1, one launch (start us, length us, event | category | flops | bytes accessed | tf_op | source)
XLA Modules:
  0.0 70.9 jit_solution(7617028454132163795)
XLA Ops:
  0.7 63.0 %slots.1 = (bf16[32,128,128]{2,1,0:T(8,128)(2,1)}, bf16[32,2,4,16,384]{4,3,2,1,0:T(8,128)(2,1)}) custom-call(s32[32]{0:T(128)} %len_ref.3, f32[1]{0:T(128)S(6)} %copy.7.scale_ref, bf16[32,128,384]{2,1,0:T(8,128)(2,1)} %tok_hbm.1, bf16[384,128]{1,0:T(8,128)(2,1)} %phi_ref.1, bf16[1,384,1536]{2,1,0:T(8,128)(2,1)} %win_hbm.1, bf16[1,1536,384]{2,1,0:T(8,128)(2,1)} %wout_hbm.1), custom_call_target="tpu_custom_call" | custom-call | tf_op jit(solution)/shard_map/slots/pallas_call | solution.py:322
  63.7 7.2 %combine.1 = bf16[32,128,384]{2,1,0:T(8,128)(2,1)} custom-call(s32[32]{0:T(128)} %len_ref.3, bf16[32,128,128]{2,1,0:T(8,128)(2,1)} %get-tuple-element.7.comb_ref, bf16[32,128,384]{2,1,0:T(8,128)(2,1)} %bitcast.1), custom_call_target="tpu_custom_call" | custom-call | tf_op jit(solution)/shard_map/combine/pallas_call | solution.py:359

commit v2 on v1

v2 whole, which is shorter than its diff:
```python
import functools

import jax
import jax.numpy as jnp
from jax import lax
from jax.experimental import pallas as pl
from jax.experimental.pallas import tpu as pltpu
from jax.sharding import PartitionSpec as P

F32, BF16 = jnp.float32, jnp.bfloat16
COLOR_ROWS = (11, 11, 10)
COLOR_START = (0, 11, 22)
COLOR_HALF = (6, 6, 5)
STRIDE = {"z": 32, "y": 8, "x": 2}
COLOR_AXES = (("z", "y", "x"), ("y", "x", "z"), ("x", "z", "y"))
COPIES = 160


def slots_kernel(
    len_ref, scale_ref, tok_hbm, phi_ref, win_hbm, wout_hbm,
    comb_hbm, gat_hbm,
    tok, win, wout, comb, part, swap, chip, relay, line,
    two_out, two_in, three_out, three_in, z_own, z_out, z_swap, z_in, lanes, gat,
    send_sem, recv_sem, local_sem,
):
    num_rows, tok_count, width = tok.shape
    me = lax.axis_index("seq")
    core = lax.rem(me, 2)
    at = {axis: lax.rem(lax.div(me, stride), 4) for axis, stride in STRIDE.items()}
    partner = me + 1 - 2 * core

    def peer(axis, step):
        return me + (lax.rem(at[axis] + step, 4) - at[axis]) * STRIDE[axis]

    copies = []

    def push(src, dst, device):
        index = len(copies)
        copy = pltpu.make_async_remote_copy(
            src_ref=src, dst_ref=dst, send_sem=send_sem.at[index], recv_sem=recv_sem.at[index],
            device_id={"seq": device}, device_id_type=pl.DeviceIdType.MESH,
        )
        copy.start()
        copies.append(copy)
        return copy

    chunks = []
    for half in range(2):
        for color in range(3):
            start, rows, cut = COLOR_START[color], COLOR_ROWS[color], COLOR_HALF[color]
            chunks.append((color, half, start + half * cut, cut if half == 0 else rows - cut))

    barrier = pltpu.get_barrier_semaphore()
    neighbours = [partner] + [peer(axis, step) for axis in STRIDE for step in (1, 2, 3)]
    for other in neighbours:
        pl.semaphore_signal(barrier, inc=1, device_id={"seq": other}, device_id_type=pl.DeviceIdType.MESH)

    loads = []
    for index, (_, _, lo, count) in enumerate(chunks):
        load = pltpu.make_async_copy(tok_hbm.at[pl.ds(lo, count)], tok.at[pl.ds(lo, count)], local_sem.at[index])
        load.start()
        loads.append(load)
    load_in = pltpu.make_async_copy(win_hbm.at[0], win, local_sem.at[6])
    load_out = pltpu.make_async_copy(wout_hbm.at[0], wout, local_sem.at[7])
    load_in.start()
    load_out.start()

    with jax.named_scope("setup"):
        params = phi_ref[...].astype(F32)
        col_inv = lax.rsqrt(jnp.sum(params * params, axis=0, keepdims=True) + 1e-6)
        phi = (params * (scale_ref[0] * col_inv)).astype(BF16)
        slot = lax.broadcasted_iota(jnp.int32, (128, 128), 0)
        place = lax.broadcasted_iota(jnp.int32, (128, 128), 1)
        phis = []
        for color in range(3):
            owner = (core + (place >> 6)) & 1
            for depth, axis in enumerate(COLOR_AXES[color]):
                owner = owner + STRIDE[axis] * ((at[axis] + (place >> (4 - 2 * depth))) & 3)
            pick = jnp.where(slot == owner, 1.0, 0.0).astype(BF16)
            phis.append(jnp.dot(phi, pick, preferred_element_type=F32).astype(BF16))
        z_own[...] = jnp.ones_like(z_own)
        position = me * tok_count + lax.broadcasted_iota(jnp.int32, (tok_count, 128), 0)
    def dispatch(chunk):
        color, _, lo, count = chunk
        xs = [tok[lo + step] for step in range(count)]
        squares = [jnp.sum(x.astype(F32) * x.astype(F32), axis=-1, keepdims=True) for x in xs]
        norms = [(x.astype(F32) * lax.rsqrt(square + 1e-6)).astype(BF16) for x, square in zip(xs, squares)]
        weights = [jnp.exp(jnp.dot(norm, phis[color], preferred_element_type=F32)) for norm in norms]
        masked = [jnp.where(position < len_ref[lo + step], weight, 0.0) for step, weight in enumerate(weights)]
        totals = [
            lax.dot_general(weight.astype(BF16), x, (((0,), (0,)), ((), ())), preferred_element_type=F32).astype(BF16)
            for weight, x in zip(masked, xs)
        ]
        for step in range(count):
            row = lo + step
            part[row, 0] = totals[step][:64]
            part[row, 1] = totals[step][64:]
            at_row = row - COLOR_START[color]
            z_own[color, at_row : at_row + 1, :] = jnp.sum(masked[step], axis=0, keepdims=True)
            comb[row] = (weights[step] / jnp.sum(weights[step], axis=-1, keepdims=True)).astype(BF16)

    def start_swap(chunk):
        color, half, lo, count = chunk
        rows = pl.ds(lo, count)
        out = [push(part.at[rows, 1], swap.at[rows], partner)]
        if half == 1:
            z_out[0, color] = pltpu.roll(z_own[color], 64, 1)
            out.append(push(z_out.at[0, color], z_swap.at[color], partner))
        return out

    def line_z(color, phase, total):
        z_out[phase, color] = total
        axis = COLOR_AXES[color][phase - 1]
        return [push(z_out.at[phase, color], z_in.at[phase - 1, color, step - 1], peer(axis, step)) for step in (1, 2, 3)]

    def sum_z(color, phase, arrivals):
        total = z_out[phase, color]
        for step in (1, 2, 3):
            arrivals[step - 1].wait_recv()
            shift = 128 - step * (64 >> (2 * phase))
            total = total + pltpu.roll(z_in[phase - 1, color, step - 1], shift, 1)
        return total

    relays, cleans, z_one = {}, {}, {}

    def start_line(chunk, arrivals):
        color, half, lo, count = chunk
        for copy in arrivals:
            copy.wait_recv()

        def body(step, carry):
            row = lo + step
            both = part[row, 0].astype(F32) + swap[row].astype(F32)
            chip[row] = both.astype(BF16).reshape(4, 16, width)
            return carry

        lax.fori_loop(0, count, body, 0)
        rows = pl.ds(lo, count)
        axis = COLOR_AXES[color][0]
        away, back = (1, 3) if half == 0 else (3, 1)
        relays[color, half] = push(chip.at[rows, 2], relay.at[rows], peer(axis, away))
        cleans[color, half] = push(chip.at[rows, back], line.at[half, rows], peer(axis, back))
        if half == 1:
            z_one[color] = line_z(color, 1, z_own[color] + z_swap[color])

    with jax.named_scope("dispatch0"):
        for chunk, load in zip(chunks[:1], loads[:1]):
            load.wait()
            dispatch(chunk)
    with jax.named_scope("barrier"):
        pl.semaphore_wait(barrier, len(neighbours))
    pending = start_swap(chunks[0])
    for index in range(len(chunks)):
        following = None
        if index + 1 < len(chunks):
            with jax.named_scope("dispatch"):
                loads[index + 1].wait()
                dispatch(chunks[index + 1])
            following = start_swap(chunks[index + 1])
        with jax.named_scope("chip"):
            start_line(chunks[index], pending)
        pending = following
    store_comb = pltpu.make_async_copy(comb, comb_hbm, local_sem.at[8])
    store_comb.start()

    seconds = {}
    for chunk in chunks:
        color, half, lo, count = chunk
        axis = COLOR_AXES[color][0]
        with jax.named_scope("relay"):
            relays[color, half].wait_recv()
            away = 1 if half == 0 else 3

            def body(step, carry):
                row = lo + step
                chip[row, away] = (chip[row, away].astype(F32) + relay[row].astype(F32)).astype(BF16)
                return carry

            lax.fori_loop(0, count, body, 0)
            rows = pl.ds(lo, count)
            seconds[color, half] = push(chip.at[rows, away], line.at[1 - half, rows], peer(axis, away))
    left = lax.broadcasted_iota(jnp.int32, (256, 256), 0)
    right = lax.broadcasted_iota(jnp.int32, (256, 256), 1)
    turn = jnp.where(((left >> 4) == (right & 15)) & ((left & 15) == (right >> 4)), 1.0, 0.0).astype(BF16)

    twos, z_two = {}, {}
    for color in range(3):
        with jax.named_scope("one"):
            rows, start = COLOR_ROWS[color], COLOR_START[color]
            span = pl.ds(start, rows)
            for half in range(2):
                cleans[color, half].wait_recv()
                seconds[color, half].wait_recv()
            z_two[color] = line_z(color, 2, sum_z(color, 1, z_one[color]))
            total = chip[span, 0].astype(F32) + line[0, span].astype(F32) + line[1, span].astype(F32)
            total = total.astype(BF16).reshape(rows * 16, width)
            turned = jnp.dot(turn[:, : rows * 16], total, preferred_element_type=F32)
            two_out[color] = turned.astype(BF16).reshape(4, 4, 16, width)
            axis = COLOR_AXES[color][1]
            twos[color] = [push(two_out.at[color, step], two_in.at[color, step - 1], peer(axis, step)) for step in (1, 2, 3)]
    threes, z_three = {}, {}
    for color in range(3):
        with jax.named_scope("two"):
            z_three[color] = line_z(color, 3, sum_z(color, 2, z_two[color]))
            total = two_out[color, 0].astype(F32)
            for step in (1, 2, 3):
                twos[color][step - 1].wait_recv()
                total = total + two_in[color, step - 1].astype(F32)
            three_out[color] = total.astype(BF16)
            axis = COLOR_AXES[color][2]
            threes[color] = [push(three_out.at[color, step], three_in.at[color, step - 1], peer(axis, step)) for step in (1, 2, 3)]
    slot_in = []
    for color in range(3):
        with jax.named_scope("three"):
            z_sum = sum_z(color, 3, z_three[color])
            total = three_out[color, 0].astype(F32)
            for step in (1, 2, 3):
                threes[color][step - 1].wait_recv()
                total = total + three_in[color, step - 1].astype(F32)
            slot_in.append((total / z_sum[:, :1]).astype(BF16))
    slot_in = jnp.concatenate(slot_in, axis=0)

    with jax.named_scope("expert"):
        load_in.wait()
        load_out.wait()
        slot_out = jnp.zeros((48, width), F32)
        for piece in range(3):
            cols = pl.ds(piece * 512, 512)
            hidden = jnp.dot(slot_in, win[:, cols], preferred_element_type=F32)
            hidden = jax.nn.gelu(hidden).astype(BF16)
            slot_out = slot_out + jnp.dot(hidden, wout[cols, :], preferred_element_type=F32)
        slot_out = slot_out.astype(BF16)
    firsts = {}
    for color in range(3):
        with jax.named_scope("first"):
            lanes[color, 0, 0] = slot_out[16 * color : 16 * color + 16]
            axis = COLOR_AXES[color][2]
            firsts[color] = [push(lanes.at[color, 0, 0], lanes.at[color, 0, 4 - step], peer(axis, step)) for step in (1, 2, 3)]
    nexts = {}
    for color in range(3):
        with jax.named_scope("next"):
            for copy in firsts[color]:
                copy.wait_recv()
            axis = COLOR_AXES[color][1]
            nexts[color] = [push(lanes.at[color, 0], lanes.at[color, 4 - step], peer(axis, step)) for step in (1, 2, 3)]
    outs, across = {}, {color: [] for color in range(3)}

    def halves(color):
        start, rows, cut = COLOR_START[color], COLOR_ROWS[color], COLOR_HALF[color]
        return pl.ds(start, cut), pl.ds(start + cut, rows - cut)

    for color in range(3):
        with jax.named_scope("turn"):
            rows, start = COLOR_ROWS[color], COLOR_START[color]
            for copy in nexts[color]:
                copy.wait_recv()
            turned = jnp.dot(turn[: rows * 16], lanes[color].reshape(256, width), preferred_element_type=F32)
            gat[pl.ds(start, rows), 0, 0] = turned.astype(BF16).reshape(rows, 16, width)
            early, late = halves(color)
            axis = COLOR_AXES[color][0]
            up, down = peer(axis, 1), peer(axis, 3)
            outs[color] = [
                push(gat.at[early, 0, 0], gat.at[early, 0, 3], up),
                push(gat.at[late, 0, 0], gat.at[late, 0, 1], down),
                push(gat.at[late, 0, 0], gat.at[late, 0, 3], up),
                push(gat.at[early, 0, 0], gat.at[early, 0, 1], down),
            ]
            span = pl.ds(start, rows)
            across[color].append(push(gat.at[span, 0, 0], gat.at[span, 1, 0], partner))
    hops = {}
    for color in range(3):
        early, late = halves(color)
        axis = COLOR_AXES[color][0]
        up, down = peer(axis, 1), peer(axis, 3)
        with jax.named_scope("hop"):
            outs[color][0].wait_recv()
            first = push(gat.at[early, 0, 3], gat.at[early, 0, 2], up)
            outs[color][1].wait_recv()
            second = push(gat.at[late, 0, 1], gat.at[late, 0, 2], down)
            hops[color] = [first, second]
            across[color].append(push(gat.at[early, 0, 3], gat.at[early, 1, 3], partner))
            across[color].append(push(gat.at[late, 0, 1], gat.at[late, 1, 1], partner))
    for color in range(3):
        early, late = halves(color)
        with jax.named_scope("late"):
            outs[color][2].wait_recv()
            across[color].append(push(gat.at[late, 0, 3], gat.at[late, 1, 3], partner))
            outs[color][3].wait_recv()
            across[color].append(push(gat.at[early, 0, 1], gat.at[early, 1, 1], partner))
    for color in range(3):
        early, late = halves(color)
        with jax.named_scope("last"):
            hops[color][0].wait_recv()
            across[color].append(push(gat.at[early, 0, 2], gat.at[early, 1, 2], partner))
            hops[color][1].wait_recv()
            across[color].append(push(gat.at[late, 0, 2], gat.at[late, 1, 2], partner))
    stores = [store_comb]
    for color in range(3):
        with jax.named_scope("store"):
            for copy in across[color]:
                copy.wait_recv()
            span = pl.ds(COLOR_START[color], COLOR_ROWS[color])
            store = pltpu.make_async_copy(gat.at[span], gat_hbm.at[span], local_sem.at[9 + color])
            store.start()
            stores.append(store)
    with jax.named_scope("drain"):
        for copy in copies:
            copy.wait_send()
        for store in stores:
            store.wait()
def combine_kernel(len_ref, comb_ref, gat_ref, y_ref):
    count, tok_count, _ = comb_ref.shape
    base = pl.program_id(0) * count
    position = lax.axis_index("seq") * tok_count + lax.broadcasted_iota(jnp.int32, (tok_count, 1), 0)
    for step in range(count):
        mixed = jnp.dot(comb_ref[step], gat_ref[step], preferred_element_type=F32).astype(BF16)
        y_ref[step] = jnp.where(position < len_ref[base + step], mixed, jnp.zeros_like(mixed))


def solution(mesh):
    def shard_body(tok_blk, len_blk, slot_params, logit_scale, w_in_blk, w_out_blk):
        rows, toks, width = tok_blk.shape
        ff = w_in_blk.shape[2]
        slots = slot_params.shape[1]
        smem = pl.BlockSpec(memory_space=pltpu.SMEM)
        vmem = pl.BlockSpec(memory_space=pltpu.VMEM)
        hbm = pl.BlockSpec(memory_space=pl.ANY)
        comb, gat = pl.pallas_call(
            slots_kernel,
            name="slots",
            out_shape=(
                jax.ShapeDtypeStruct((rows, toks, slots), BF16),
                jax.ShapeDtypeStruct((rows, 2, 4, 16, width), BF16),
            ),
            in_specs=[smem, smem, hbm, vmem, hbm, hbm],
            out_specs=(hbm, hbm),
            scratch_shapes=[
                pltpu.VMEM((rows, toks, width), BF16),
                pltpu.VMEM((width, ff), BF16),
                pltpu.VMEM((ff, width), BF16),
                pltpu.VMEM((rows, toks, slots), BF16),
                pltpu.VMEM((rows, 2, 64, width), BF16),
                pltpu.VMEM((rows, 64, width), BF16),
                pltpu.VMEM((rows, 4, 16, width), BF16),
                pltpu.VMEM((rows, 16, width), BF16),
                pltpu.VMEM((2, rows, 16, width), BF16),
                pltpu.VMEM((3, 4, 4, 16, width), BF16),
                pltpu.VMEM((3, 3, 4, 16, width), BF16),
                pltpu.VMEM((3, 4, 16, width), BF16),
                pltpu.VMEM((3, 3, 16, width), BF16),
                pltpu.VMEM((3, 16, slots), F32),
                pltpu.VMEM((4, 3, 16, slots), F32),
                pltpu.VMEM((3, 16, slots), F32),
                pltpu.VMEM((3, 3, 3, 16, slots), F32),
                pltpu.VMEM((3, 4, 4, 16, width), BF16),
                pltpu.VMEM((rows, 2, 4, 16, width), BF16),
                pltpu.SemaphoreType.DMA((COPIES,)),
                pltpu.SemaphoreType.DMA((COPIES,)),
                pltpu.SemaphoreType.DMA((12,)),
            ],
            compiler_params=pltpu.CompilerParams(collective_id=0, has_side_effects=True, vmem_limit_bytes=60 * 1024 * 1024),
        )(len_blk, logit_scale, tok_blk, slot_params, w_in_blk, w_out_blk)
        gat = gat.reshape(rows, slots, width)
        block = 4
        return pl.pallas_call(
            combine_kernel,
            name="combine",
            out_shape=jax.ShapeDtypeStruct((rows, toks, width), BF16),
            grid=(rows // block,),
            in_specs=[
                smem,
                pl.BlockSpec((block, toks, slots), lambda i: (i, 0, 0)),
                pl.BlockSpec((block, slots, width), lambda i: (i, 0, 0)),
            ],
            out_specs=pl.BlockSpec((block, toks, width), lambda i: (i, 0, 0)),
        )(len_blk, comb, gat)

    return jax.shard_map(
        shard_body,
        mesh=mesh,
        in_specs=(P("data", "seq", None), P("data"), P(None, None), P(None), P("seq", None, None), P("seq", None, None)),
        out_specs=P("data", "seq", None),
        check_vma=False,
    )
```

time: 71.2 us -> 62.8 us (0.88)
  Pallas kernels: 70.2 us -> 61.9 us
    pallas_call x1, Pallas kernels: 63 us -> 54.6 us  [shard_body(): pl.pallas_call(slots_kernel, name='slots', out_shape=(jax.ShapeDtypeStruc...]
where the time goes in v2:
time: 62.8 us; the launch traced here: 62.5 us
  Pallas kernels  61.9 us (99%)
  between operations  0.66 us (1%)
    pallas_call x1, Pallas kernels, shard_body(): pl.pallas_call(slots_kernel, name='slots', out_shape=(jax.ShapeDtypeStruc...  54.6 us
    pallas_call x1, Pallas kernels, shard_body(): pl.pallas_call(combine_kernel, name='combine', out_shape=jax.ShapeDtypeSt...  7.23 us

profile of v2, /device:TPU:1, one launch (start us, length us, event | category | flops | bytes accessed | tf_op | source)
XLA Modules:
  0.0 62.5 jit_solution(6556877854855937099)
XLA Ops:
  0.7 54.6 %slots.1 = (bf16[32,128,128]{2,1,0:T(8,128)(2,1)}, bf16[32,2,4,16,384]{4,3,2,1,0:T(8,128)(2,1)}) custom-call(s32[32]{0:T(128)} %len_ref.3, f32[1]{0:T(128)S(6)} %copy.7.scale_ref, bf16[32,128,384]{2,1,0:T(8,128)(2,1)} %tok_hbm.1, bf16[384,128]{1,0:T(8,128)(2,1)} %phi_ref.1, bf16[1,384,1536]{2,1,0:T(8,128)(2,1)} %win_hbm.1, bf16[1,1536,384]{2,1,0:T(8,128)(2,1)} %wout_hbm.1), custom_call_target="tpu_custom_call" | custom-call | tf_op jit(solution)/shard_map/slots/pallas_call | solution.py:328
  55.3 7.2 %combine.1 = bf16[32,128,384]{2,1,0:T(8,128)(2,1)} custom-call(s32[32]{0:T(128)} %len_ref.3, bf16[32,128,128]{2,1,0:T(8,128)(2,1)} %get-tuple-element.7.comb_ref, bf16[32,128,384]{2,1,0:T(8,128)(2,1)} %bitcast.1), custom_call_target="tpu_custom_call" | custom-call | tf_op jit(solution)/shard_map/combine/pallas_call | solution.py:365

commit v3 on v2

--- a/solution.py
+++ b/solution.py
@@ -18,9 +18,9 @@
 
 def slots_kernel(
     len_ref, scale_ref, tok_hbm, phi_ref, win_hbm, wout_hbm,
-    comb_hbm, gat_hbm,
-    tok, win, wout, comb, part, swap, chip, relay, line,
-    two_out, two_in, three_out, three_in, z_own, z_out, z_swap, z_in, lanes, gat,
+    comb, gat,
+    tok, win, wout, part, swap, chip, relay, line,
+    two_out, two_in, three_out, three_in, z_own, z_out, z_swap, z_in, lanes,
     send_sem, recv_sem, local_sem,
 ):
     num_rows, tok_count, width = tok.shape
@@ -160,8 +160,6 @@
         with jax.named_scope("chip"):
             start_line(chunks[index], pending)
         pending = following
-    store_comb = pltpu.make_async_copy(comb, comb_hbm, local_sem.at[8])
-    store_comb.start()
 
     seconds = {}
     for chunk in chunks:
@@ -294,27 +292,30 @@
             across[color].append(push(gat.at[early, 0, 2], gat.at[early, 1, 2], partner))
             hops[color][1].wait_recv()
             across[color].append(push(gat.at[late, 0, 2], gat.at[late, 1, 2], partner))
-    stores = [store_comb]
-    for color in range(3):
-        with jax.named_scope("store"):
+    with jax.named_scope("across"):
+        for color in range(3):
             for copy in across[color]:
                 copy.wait_recv()
-            span = pl.ds(COLOR_START[color], COLOR_ROWS[color])
-            store = pltpu.make_async_copy(gat.at[span], gat_hbm.at[span], local_sem.at[9 + color])
-            store.start()
-            stores.append(store)
     with jax.named_scope("drain"):
         for copy in copies:
             copy.wait_send()
-        for store in stores:
-            store.wait()
-def combine_kernel(len_ref, comb_ref, gat_ref, y_ref):
-    count, tok_count, _ = comb_ref.shape
-    base = pl.program_id(0) * count
+
+
+def combine_kernel(len_ref, comb, gat, y_hbm, y, sem):
+    num_rows, tok_count, width = y.shape
     position = lax.axis_index("seq") * tok_count + lax.broadcasted_iota(jnp.int32, (tok_count, 1), 0)
-    for step in range(count):
-        mixed = jnp.dot(comb_ref[step], gat_ref[step], preferred_element_type=F32).astype(BF16)
-        y_ref[step] = jnp.where(position < len_ref[base + step], mixed, jnp.zeros_like(mixed))
+    group = 4
+    stores = []
+    for first in range(0, num_rows, group):
+        for row in range(first, first + group):
+            mixed = jnp.dot(comb[row], gat[row].reshape(128, width), preferred_element_type=F32).astype(BF16)
+            y[row] = jnp.where(position < len_ref[row], mixed, jnp.zeros_like(mixed))
+        span = pl.ds(first, group)
+        store = pltpu.make_async_copy(y.at[span], y_hbm.at[span], sem.at[first // group])
+        store.start()
+        stores.append(store)
+    for store in stores:
+        store.wait()
 
 
 def solution(mesh):
@@ -324,21 +325,20 @@
         slots = slot_params.shape[1]
         smem = pl.BlockSpec(memory_space=pltpu.SMEM)
         vmem = pl.BlockSpec(memory_space=pltpu.VMEM)
-        hbm = pl.BlockSpec(memory_space=pl.ANY)
+        hbm = pl.BlockSpec(memory_space=pltpu.HBM)
         comb, gat = pl.pallas_call(
             slots_kernel,
             name="slots",
             out_shape=(
-                jax.ShapeDtypeStruct((rows, toks, slots), BF16),
-                jax.ShapeDtypeStruct((rows, 2, 4, 16, width), BF16),
+                pltpu.VMEM((rows, toks, slots), BF16),
+                pltpu.VMEM((rows, 2, 4, 16, width), BF16),
             ),
             in_specs=[smem, smem, hbm, vmem, hbm, hbm],
-            out_specs=(hbm, hbm),
+            out_specs=(vmem, vmem),
             scratch_shapes=[
                 pltpu.VMEM((rows, toks, width), BF16),
                 pltpu.VMEM((width, ff), BF16),
                 pltpu.VMEM((ff, width), BF16),
-                pltpu.VMEM((rows, toks, slots), BF16),
                 pltpu.VMEM((rows, 2, 64, width), BF16),
                 pltpu.VMEM((rows, 64, width), BF16),
                 pltpu.VMEM((rows, 4, 16, width), BF16),
@@ -353,26 +353,20 @@
                 pltpu.VMEM((3, 16, slots), F32),
                 pltpu.VMEM((3, 3, 3, 16, slots), F32),
                 pltpu.VMEM((3, 4, 4, 16, width), BF16),
-                pltpu.VMEM((rows, 2, 4, 16, width), BF16),
                 pltpu.SemaphoreType.DMA((COPIES,)),
                 pltpu.SemaphoreType.DMA((COPIES,)),
-                pltpu.SemaphoreType.DMA((12,)),
+                pltpu.SemaphoreType.DMA((8,)),
             ],
-            compiler_params=pltpu.CompilerParams(collective_id=0, has_side_effects=True, vmem_limit_bytes=60 * 1024 * 1024),
+            compiler_params=pltpu.CompilerParams(collective_id=0, has_side_effects=True, vmem_limit_bytes=56 * 1024 * 1024),
         )(len_blk, logit_scale, tok_blk, slot_params, w_in_blk, w_out_blk)
-        gat = gat.reshape(rows, slots, width)
-        block = 4
         return pl.pallas_call(
             combine_kernel,
             name="combine",
             out_shape=jax.ShapeDtypeStruct((rows, toks, width), BF16),
-            grid=(rows // block,),
-            in_specs=[
-                smem,
-                pl.BlockSpec((block, toks, slots), lambda i: (i, 0, 0)),
-                pl.BlockSpec((block, slots, width), lambda i: (i, 0, 0)),
-            ],
-            out_specs=pl.BlockSpec((block, toks, width), lambda i: (i, 0, 0)),
+            in_specs=[smem, vmem, vmem],
+            out_specs=hbm,
+            scratch_shapes=[pltpu.VMEM((rows, toks, width), BF16), pltpu.SemaphoreType.DMA((8,))],
+            compiler_params=pltpu.CompilerParams(vmem_limit_bytes=16 * 1024 * 1024),
         )(len_blk, comb, gat)
 
     return jax.shard_map(

time: 62.8 us -> 57 us (0.908)
  Pallas kernels: 61.9 us -> 56.2 us
    pallas_call x1, Pallas kernels: 7.23 us -> 2.52 us  [shard_body(): pl.pallas_call(combine_kernel, name='combine', out_shape=jax.ShapeDtypeSt...]
    pallas_call x1, Pallas kernels: 54.6 us -> 53.6 us  [shard_body(): pl.pallas_call(slots_kernel, name='slots', out_shape=(pltpu.VMEM((rows, t...]
where the time goes in v3:
time: 57 us; the launch traced here: 56.8 us
  Pallas kernels  56.2 us (99%)
  between operations  0.68 us (1%)
    pallas_call x1, Pallas kernels, shard_body(): pl.pallas_call(slots_kernel, name='slots', out_shape=(pltpu.VMEM((rows, t...  53.6 us
    pallas_call x1, Pallas kernels, shard_body(): pl.pallas_call(combine_kernel, name='combine', out_shape=jax.ShapeDtypeSt...  2.52 us

profile of v3, /device:TPU:1, one launch (start us, length us, event | category | flops | bytes accessed | tf_op | source)
XLA Modules:
  0.0 56.8 jit_solution(12792641191592917507)
XLA Ops:
  0.0 0.0 copy-start
  0.7 53.6 %slots.1 = (bf16[32,128,128]{2,1,0:T(8,128)(2,1)S(1)}, bf16[32,2,4,16,384]{4,3,2,1,0:T(8,128)(2,1)S(1)}) custom-call(s32[32]{0:T(128)} %len_ref.3, f32[1]{0:T(128)S(6)} %copy.7.scale_ref, bf16[32,128,384]{2,1,0:T(8,128)(2,1)} %tok_hbm.1, bf16[384,128]{1,0:T(8,128)(2,1)} %phi_ref.1, bf16[1,384,1536]{2,1,0:T(8,128)(2,1)} %win_hbm.1, bf16[1,1536,384]{2,1,0:T(8,128)(2,1)} %wout_hbm.1), custom_call_target="tpu_custom_call" | custom-call | tf_op jit(solution)/shard_map/slots/pallas_call | solution.py:329
  54.3 0.0 copy-done
  54.3 2.5 %combine.1 = bf16[32,128,384]{2,1,0:T(8,128)(2,1)} custom-call(s32[32]{0:T(128)S(1)} %copy-done, bf16[32,128,128]{2,1,0:T(8,128)(2,1)S(1)} %get-tuple-element.7.comb, bf16[32,2,4,16,384]{4,3,2,1,0:T(8,128)(2,1)S(1)} %get-tuple-element.8.gat), custom_call_target="tpu_custom_call" | custom-call | tf_op jit(solution)/shard_map/combine/pallas_call | solution.py:362
Async XLA Ops:
  0.0 54.3 %copy-start = (s32[32]{0:T(128)S(1)}, s32[32]{0:T(128)}, u32[]{:S(2)}) copy-start(s32[32]{0:T(128)} %len_ref.3) | copy-start | bytes 388
